TPU v7x, 32 devices: a whole 2x2x4 slice. The times are simulated.
32 devices in a mesh: groups: 2 (over y), ep: 16 (over z, x, core).
Axes of the slice: x: 2, y: 2, z: 4, core: 2. Of those that a mesh axis runs over, the one named last changes fastest.
Arguments:
- tokens: bfloat16 [4096, 1440], P(('groups', 'ep')), parts along dimension 0, may hold values from -6 to 6
- expert_ids: int32 [4096, 4], P(('groups', 'ep')), parts along dimension 0, may hold values from 0 to 15, as said below
- combine: float32 [4096, 4], P(('groups', 'ep')), parts along dimension 0, may hold values from 0.05 to 1
- gate_weight: bfloat16 [16, 1440, 1440], P('ep'), may hold values from -0.15625 to 0.15625
- up_weight: bfloat16 [16, 1440, 1440], P('ep'), may hold values from -0.15625 to 0.15625
- down_weight: bfloat16 [16, 1440, 1440], P('ep'), may hold values from -0.15625 to 0.15625
Outputs:
- mixture: bfloat16 [4096, 1440], P(('groups', 'ep')), parts along dimension 0
There are 2 independent parts, one for each index of `groups`. A program takes and returns all parts, laid end to end along the dimension named above; an argument that names none is the same for every part. Nothing has to cross between parts.
Inputs may be any that keep to these rules, and one draw needn't show every extreme that they name: `expert_ids`: each row names 4 different experts. In the rows of one device (aligned blocks of 128 rows) no expert is named more than 64 times, and some expert is named exactly 64 times in every block.
All inputs are finite; a program needn't handle non-finite values.
Results may differ from a plain program's by a relative error of at most 0.0058.
Values may be sent and summed in bfloat16 or wider, within the bound.
A program may use at most 64 MiB of HBM per device.

v0:
```python
import jax
import jax.numpy as jnp
from jax import lax
from jax.sharding import PartitionSpec as P

alpha_gate = 1.702


def run_expert_block(row_block, gate_proj, up_proj, down_proj):
    gate_part = jnp.dot(row_block, gate_proj, preferred_element_type=jnp.float32)
    up_part = jnp.dot(row_block, up_proj, preferred_element_type=jnp.float32)
    hidden = ((up_part + 1.0) * gate_part * jax.nn.sigmoid(alpha_gate * gate_part)).astype(
        jnp.bfloat16
    )
    return jnp.dot(hidden, down_proj, preferred_element_type=jnp.float32).astype(jnp.bfloat16)


def on_device(tokens, expert_ids, combine, gate_weight, up_weight, down_weight):
    members = lax.axis_size("ep")
    tokens_here, fanout = expert_ids.shape
    features = tokens.shape[1]
    capacity = 2 * tokens_here * fanout // members
    received_rows = members * capacity
    flat_ids = expert_ids.reshape(-1)
    onehot = (flat_ids[:, None] == jnp.arange(members, dtype=jnp.int32)[None, :]).astype(jnp.int32)
    running = jnp.cumsum(onehot, axis=0) - onehot
    slot_rank = jnp.sum(running * onehot, axis=1)
    target = flat_ids * capacity + slot_rank
    source_token = jnp.arange(tokens_here * fanout, dtype=jnp.int32) // fanout
    outgoing = (
        jnp.zeros((received_rows, features), jnp.bfloat16).at[target].set(tokens[source_token])
    )
    outgoing = outgoing.reshape(members, capacity, features)
    gate_proj, up_proj, down_proj = (gate_weight[0], up_weight[0], down_weight[0])
    arrived = lax.all_to_all(outgoing, "ep", split_axis=0, concat_axis=0, tiled=True)
    shape_here = arrived.shape
    answers = run_expert_block(
        arrived.reshape(-1, features), gate_proj, up_proj, down_proj
    ).reshape(shape_here)
    returned = lax.all_to_all(answers, "ep", split_axis=0, concat_axis=0, tiled=True)
    selected_experts = (
        returned.reshape(-1, features)[target]
        .astype(jnp.float32)
        .reshape(tokens_here, fanout, features)
    )
    mixture = jnp.sum(selected_experts * combine[:, :, None], axis=1)
    return mixture.astype(jnp.bfloat16)


def solution(mesh):
    in_specs = (
        P(("groups", "ep"), None),
        P(("groups", "ep"), None),
        P(("groups", "ep"), None),
        P("ep", None, None),
        P("ep", None, None),
        P("ep", None, None),
    )
    out_specs = P(("groups", "ep"), None)
    return jax.shard_map(
        on_device, mesh=mesh, in_specs=in_specs, out_specs=out_specs, check_vma=False
    )
```

profile of v0, /device:TPU:8, one launch (start us, length us, event | category | flops | bytes accessed | tf_op | source)
XLA Modules:
  0.0 201.8 jit_solution(2135248783991042265)
XLA Ops:
  0.0 0.8 copy.26
  0.8 0.1 eq.29
  0.9 0.1 eq.25
  1.0 0.7 broadcast_multiply_fusion
  1.7 1.2 reduce-window.6
  2.9 0.2 slice_reduce_fusion
  3.1 0.1 copy.25
  3.2 0.1 mul.41
  3.4 1.2 copy.29
  4.5 0.1 fusion.22
  4.6 9.2 %scatter_custom_fusion = bf16[1024,1440]{1,0:T(8,128)(2,1)S(1)} fusion(s32[512]{0:T(512)S(1)} %bitcast.50, bf16[128,1440]{1,0:T(8,128)(2,1)S(1)} %copy.29, s32[1024]{0:T(1024)S(1)} %pad_clamp_fusion.1, bf16[]{:T(256)} %constant.26.clone.1), kind=kCustom, calls=%fused_computation.14 | custom fusion | bytes 2949122 | tf_op jit(solution)/shard_map/scatter | solution.py:31
  13.8 0.0 copy-start.2
  13.8 76.0 %all_to_all.10 = bf16[16,64,1440]{2,1,0:T(8,128)(2,1)S(1)} all-to-all(bf16[16,64,1440]{2,1,0:T(8,128)(2,1)S(1)} %bitcast.47), channel_id=1, replica_groups=mesh['groups'=2,'ep'=16] {'ep'}, dimensions={0} | all-to-all | bytes 5898240 | tf_op jit(solution)/shard_map/all_to_all | solution.py:35
  89.8 1.7 copy-done
  91.5 6.7 %fusion.8 = f32[1024,1440]{0,1:T(8,128)} fusion(bf16[1024,1440]{1,0:T(8,128)(2,1)S(1)} %bitcast.48, bf16[1,1440,1440]{2,1,0:T(8,128)(2,1)S(1)} %copy-done.2), kind=kOutput, calls=%fused_computation.8 | convolution fusion | flops 4246732800 | bytes 12994560 | tf_op jit(solution)/shard_map/dot_general | solution.py:11
  98.2 17.1 %fusion.10 = bf16[1024,1440]{0,1:T(8,128)(2,1)S(1)} fusion(bf16[1,1440,1440]{2,1,0:T(8,128)(2,1)} %param.11, f32[1024,1440]{0,1:T(8,128)} %fusion.8, bf16[1024,1440]{1,0:T(8,128)(2,1)} %bitcast.49, bf16[1,1440,1440]{2,1,0:T(8,128)(2,1)} %param.9), kind=kOutput, calls=%fused_computation.10 | convolution fusion | flops 8506736640 | bytes 20090880 | tf_op jit(solution)/shard_map/dot_general | solution.py:15
  115.3 2.9 %copy.30 = bf16[1024,1440]{1,0:T(8,128)(2,1)} copy(bf16[1024,1440]{0,1:T(8,128)(2,1)S(1)} %fusion.10) | data formatting | bytes 5898240 | tf_op jit(solution)/shard_map/convert_element_type | solution.py:15
  118.2 5.3 %all-to-all-start.1 = ((bf16[16,64,1440]{2,1,0:T(8,128)(2,1)}), bf16[16,64,1440]{2,1,0:T(8,128)(2,1)S(1)}, u32[]{:S(2)}, u32[]{:S(2)}) async-start(bf16[16,64,1440]{2,1,0:T(8,128)(2,1)} %bitcast.46), calls=%async_computation.1 | async-start | bytes 6291456 | tf_op jit(solution)/shard_map/all_to_all | solution.py:40
  123.6 0.7 copy.31
  124.3 67.6 %all-to-all-done.1 = bf16[16,64,1440]{2,1,0:T(8,128)(2,1)S(1)} async-done(((bf16[16,64,1440]{2,1,0:T(8,128)(2,1)}), bf16[16,64,1440]{2,1,0:T(8,128)(2,1)S(1)}, u32[]{:S(2)}, u32[]{:S(2)}) %all-to-all-start.1) | async-done | bytes 2949152 | tf_op jit(solution)/shard_map/all_to_all | solution.py:40
  191.9 3.0 %gather_fusion = bf16[512,1440]{1,0:T(8,128)(2,1)} fusion(bf16[1024,1440]{1,0:T(8,128)(2,1)S(1)} %bitcast.45, s32[1024]{0:T(1024)S(1)} %pad_clamp_fusion), kind=kCustom, calls=%fused_computation.1 | custom fusion | bytes 2951168 | tf_op jit(solution)/shard_map/gather | solution.py:42
  194.8 2.9 %reshape.111 = f32[128,4,1440]{2,1,0:T(4,128)S(1)} reshape(bf16[512,1440]{1,0:T(8,128)(2,1)} %gather_fusion) | data formatting | bytes 4423680 | tf_op jit(solution)/shard_map/convert_element_type | solution.py:43
  197.7 3.1 %multiply_reduce_fusion = bf16[128,1440]{1,0:T(8,128)(2,1)S(1)} fusion(f32[128,4,1440]{2,1,0:T(4,128)S(1)} %reshape.111, f32[128,4]{1,0:T(8,128)} %copy.31), kind=kLoop, calls=%fused_computation.11 | loop fusion | flops 1290240 | bytes 3319808 | tf_op jit(solution)/shard_map/reduce_sum | solution.py:46
  200.9 0.9 copy.32
  (11 shorter events, 0.1 us)
Async XLA Ops:
  13.8 77.7 %copy-start.2 = (bf16[1,1440,1440]{2,1,0:T(8,128)(2,1)S(1)}, bf16[1,1440,1440]{2,1,0:T(8,128)(2,1)}, u32[]{:S(2)}) copy-start(bf16[1,1440,1440]{2,1,0:T(8,128)(2,1)} %param.10) | copy-start | bytes 12441604
  89.8 1.7 copy-start
  118.2 5.3 %copy-start.1 = (f32[128,4]{0,1:T(4,128)S(1)}, f32[128,4]{0,1:T(4,128)}, u32[]{:S(2)}) copy-start(f32[128,4]{0,1:T(4,128)} %param.8) | copy-start | bytes 6148
  118.2 73.6 %all-to-all-start.1 = ((bf16[16,64,1440]{2,1,0:T(8,128)(2,1)}), bf16[16,64,1440]{2,1,0:T(8,128)(2,1)S(1)}, u32[]{:S(2)}, u32[]{:S(2)}) async-start(bf16[16,64,1440]{2,1,0:T(8,128)(2,1)} %bitcast.46), calls=%async_computation.1 | async-start | bytes 6291456 | tf_op jit(solution)/shard_map/all_to_all | solution.py:40
where the time goes:
time: 204 us; the launch traced here: 202 us
  blocking collectives  76 us (37%)
  waiting for transfers between devices  67.6 us (33%)
  local copies, waits for them, and re-layouts  24 us (12%)
  matrix products  23.8 us (12%)
  starting transfers between devices  5.32 us (3%)
  other arithmetic  5.14 us (3%)
    all_to_all x1, blocking collectives, on_device(): lax.all_to_all(outgoing, 'ep', split_axis=0, concat_axis=0, tiled=True)  76 us
    all_to_all x1, waiting for transfers between devices, on_device(): lax.all_to_all(answers, 'ep', split_axis=0, concat_axis=0, tiled=True)  67.6 us
    dot_general x1, matrix products, run_expert_block(): jnp.dot(hidden, down_proj, preferred_element_type=jnp.float32)  17.1 us
    scatter x1, local copies, waits for them, and re-layouts, on_device(): jnp.zeros((received_rows, features), jnp.bfloat16).at[target]  9.15 us
    dot_general x1, matrix products, run_expert_block(): up_part = jnp.dot(row_block, up_proj, preferred_element_type=jnp.float32)  6.68 us
    all_to_all x1, starting transfers between devices, on_device(): lax.all_to_all(answers, 'ep', split_axis=0, concat_axis=0, tiled=True)  5.32 us
    unnamed x9, local copies, waits for them, and re-layouts  4.42 us
  transfers between devices with their start and end apart: 1, of which 1 were waited for; matrix products, arithmetic and copies ran while one was open for 0% of the time, Pallas kernels for 0%

commit v1 on v0

--- a/solution.py
+++ b/solution.py
@@ -1,7 +1,13 @@
+import functools
+
 import jax
 import jax.numpy as jnp
 from jax import lax
+from jax.experimental import pallas as pl
+from jax.experimental.pallas import tpu as pltpu
 from jax.sharding import PartitionSpec as P
+
+MESH = pl.DeviceIdType.MESH
 
 alpha_gate = 1.702
 
@@ -13,6 +19,301 @@
         jnp.bfloat16
     )
     return jnp.dot(hidden, down_proj, preferred_element_type=jnp.float32).astype(jnp.bfloat16)
+
+
+def line_kernel(
+    tok_hbm, mix_ref, gate_hbm, up_hbm, down_hbm, out_ref,
+    x_buf, w_in, gate_w, up_w, down_w, rows, part, other, quad, rx, ru, rd,
+    load_sem, agz_s, agx_s, agp_s, w_s, pc_s, rsx_s, rsz_s,
+    x_r, w_r, q_r, rx_r, ru_r, rd_r,
+    *, members, capacity,
+):
+    length = members // 4
+    here = tok_hbm.shape[0]
+    me = lax.axis_index("ep")
+    z, x, c = me // 4, (me // 2) % 2, me % 2
+    pc = 1 - c
+
+    def member(zz, xx, cc):
+        return (zz * 2 + xx) * 2 + cc
+
+    across = member(z, 1 - x, c)
+    partner = member(z, x, pc)
+    above = member(jnp.minimum(z + 1, length - 1), x, c)
+    below = member(jnp.maximum(z - 1, 0), x, c)
+
+    def send(src, dst, ssem, rsem, to):
+        return pltpu.make_async_remote_copy(
+            src_ref=src, dst_ref=dst, send_sem=ssem, recv_sem=rsem,
+            device_id={"ep": to}, device_id_type=MESH,
+        )
+
+    loads = [
+        pltpu.make_async_copy(tok_hbm, x_buf.at[z, x, c], load_sem.at[0]),
+        pltpu.make_async_copy(gate_hbm, gate_w, load_sem.at[1]),
+        pltpu.make_async_copy(up_hbm, up_w, load_sem.at[2]),
+        pltpu.make_async_copy(down_hbm, down_w, load_sem.at[3]),
+    ]
+    for load in loads:
+        load.start()
+
+    barrier = pltpu.get_barrier_semaphore()
+    for step in range(1, members):
+        to = lax.rem(me + step, members)
+        pl.semaphore_signal(barrier, inc=1, device_id={"ep": to}, device_id_type=MESH)
+    pl.semaphore_wait(barrier, members - 1)
+
+    def weights_copy(step):
+        to = lax.rem(me + step, members)
+        return send(mix_ref.at[to], w_in.at[me], w_s.at[step], w_r.at[me], to)
+
+    def weights_arrival(step):
+        origin = lax.rem(me + step, members)
+        return send(mix_ref.at[origin], w_in.at[origin], w_s.at[step], w_r.at[origin], origin)
+
+    def ag(zz, xx, ssem, to):
+        slot = x_buf.at[zz, xx, c]
+        return send(slot, slot, ssem, x_r.at[zz, xx, c], to)
+
+    def to_above(zz):
+        return ag(zz, x, agz_s.at[zz, 0], above)
+
+    def to_below(zz):
+        return ag(zz, x, agz_s.at[zz, 1], below)
+
+    def to_across(zz):
+        return ag(zz, x, agx_s.at[zz], across)
+
+    def to_partner(zz, xx):
+        return ag(zz, xx, agp_s.at[zz, xx], partner)
+
+    def goes_up(zz):
+        return jnp.logical_and(zz <= z, z < length - 1)
+
+    def goes_down(zz):
+        return jnp.logical_and(zz >= z, z > 0)
+
+    def forward(zz):
+        @pl.when(goes_up(zz))
+        def _():
+            to_above(zz).start()
+
+        @pl.when(goes_down(zz))
+        def _():
+            to_below(zz).start()
+
+        to_across(zz).start()
+        to_partner(zz, x).start()
+
+    def arrival(zz, xx, cc):
+        slot = x_buf.at[zz, xx, cc]
+        send(slot, slot, agx_s.at[zz], x_r.at[zz, xx, cc], partner).wait_recv()
+
+    near = jnp.minimum(z, length - 1 - z)
+
+    def nearest(k):
+        along = near + jnp.where(k % 2 == 1, (k + 1) // 2, -(k // 2))
+        low = jnp.where(k <= 2 * near, along, k)
+        return jnp.where(z == near, low, length - 1 - low)
+
+    loads[0].wait()
+    forward(z)
+    for step in range(1, members):
+        weights_copy(step).start()
+    w_in[me] = mix_ref[me]
+    for step in range(1, members):
+        weights_arrival(step).wait_recv()
+
+    row_at = lax.broadcasted_iota(jnp.int32, (capacity, here), 0).astype(jnp.float32)
+    before = (
+        lax.broadcasted_iota(jnp.int32, (here, here), 0)
+        < lax.broadcasted_iota(jnp.int32, (here, here), 1)
+    ).astype(jnp.bfloat16)
+
+    def picker(zz, xx, cc):
+        weight = w_in[member(zz, xx, cc)]
+        named = weight > 0.0
+        flags = jnp.broadcast_to(named.astype(jnp.float32), (8, here)).astype(jnp.bfloat16)
+        rank = jnp.dot(flags, before, preferred_element_type=jnp.float32)[0:1, :]
+        pick = jnp.where(named, rank, -1.0) == row_at
+        scale = jnp.sum(jnp.where(pick, weight, 0.0), axis=1, keepdims=True)
+        return pick.astype(jnp.float32).astype(jnp.bfloat16), scale
+
+    def compute(zz, xx):
+        picks, scales = [], []
+        for side, cc in enumerate((c, pc)):
+            pick, scale = picker(zz, xx, cc)
+            picks.append(pick)
+            scales.append(scale)
+            rows[side * capacity : (side + 1) * capacity, :] = jnp.dot(
+                pick, x_buf[zz, xx, cc], preferred_element_type=jnp.float32
+            ).astype(jnp.bfloat16)
+        block = rows[...]
+        gate = jnp.dot(block, gate_w[...], preferred_element_type=jnp.float32)
+        up = jnp.dot(block, up_w[...], preferred_element_type=jnp.float32)
+        hidden = ((up + 1.0) * gate * jax.nn.sigmoid(alpha_gate * gate)).astype(jnp.bfloat16)
+        answer = jnp.dot(hidden, down_w[...], preferred_element_type=jnp.float32)
+        for side, dst in enumerate((part, other)):
+            scaled = (
+                answer[side * capacity : (side + 1) * capacity, :]
+                .astype(jnp.bfloat16).astype(jnp.float32) * scales[side]
+            ).astype(jnp.bfloat16)
+            dst[zz, xx] = lax.dot_general(
+                picks[side], scaled, (((0,), (0,)), ((), ())),
+                preferred_element_type=jnp.float32,
+            ).astype(jnp.bfloat16)
+
+    def answer_copy(zz, xx):
+        return send(other.at[zz, xx], quad.at[zz, xx], pc_s.at[zz, xx], q_r.at[zz, xx], partner)
+
+    def across_copy(zz):
+        return send(part.at[zz, 1 - x], rx.at[zz], rsx_s.at[zz], rx_r.at[zz], across)
+
+    def join_partner(zz, xx):
+        answer_copy(zz, xx).wait_recv()
+        part[zz, xx] = (
+            part[zz, xx].astype(jnp.float32) + quad[zz, xx].astype(jnp.float32)
+        ).astype(jnp.bfloat16)
+
+    for load in loads[1:]:
+        load.wait()
+
+    def step_of(i, carry):
+        k, o = i // 2, i % 2
+        zz, xx = nearest(k), (x + o) % 2
+
+        @pl.when(o == 1)
+        def _():
+            @pl.when(k + 1 < length)
+            def _():
+                following = nearest(k + 1)
+                arrival(following, x, c)
+                forward(following)
+
+            arrival(zz, 1 - x, c)
+            to_partner(zz, 1 - x).start()
+
+        arrival(zz, xx, pc)
+        compute(zz, xx)
+        answer_copy(zz, xx).start()
+
+        @pl.when(i > 0)
+        def _():
+            last = nearest((i - 1) // 2)
+            last_x = (x + (i - 1) % 2) % 2
+            join_partner(last, last_x)
+
+            @pl.when(o == 0)
+            def _():
+                across_copy(last).start()
+
+        return carry
+
+    lax.fori_loop(0, 2 * length, step_of, 0)
+    final = nearest(length - 1)
+    join_partner(final, 1 - x)
+    across_copy(final).start()
+
+    def up_copy(zz):
+        return send(part.at[zz, x], ru.at[zz], rsz_s.at[zz], ru_r.at[zz], above)
+
+    def down_copy(zz):
+        return send(part.at[zz, x], rd.at[zz], rsz_s.at[zz], rd_r.at[zz], below)
+
+    def chain(i, carry):
+        zz = nearest(length - 1 - i)
+        across_copy(zz).wait_recv()
+        total = part[zz, x].astype(jnp.float32) + rx[zz].astype(jnp.float32)
+        part[zz, x] = total.astype(jnp.bfloat16)
+
+        @pl.when(jnp.logical_and(zz >= z, z > 0))
+        def _():
+            up_copy(zz).wait_recv()
+            part[zz, x] = (
+                part[zz, x].astype(jnp.float32) + ru[zz].astype(jnp.float32)
+            ).astype(jnp.bfloat16)
+
+        @pl.when(jnp.logical_and(zz <= z, z < length - 1))
+        def _():
+            down_copy(zz).wait_recv()
+            part[zz, x] = (
+                part[zz, x].astype(jnp.float32) + rd[zz].astype(jnp.float32)
+            ).astype(jnp.bfloat16)
+
+        @pl.when(zz > z)
+        def _():
+            up_copy(zz).start()
+
+        @pl.when(zz < z)
+        def _():
+            down_copy(zz).start()
+
+        return carry
+
+    lax.fori_loop(0, length, chain, 0)
+    out_ref[...] = part[z, x]
+
+    for step in range(1, members):
+        weights_copy(step).wait_send()
+
+    def drain(zz, carry):
+        @pl.when(goes_up(zz))
+        def _():
+            to_above(zz).wait_send()
+
+        @pl.when(goes_down(zz))
+        def _():
+            to_below(zz).wait_send()
+
+        to_across(zz).wait_send()
+        across_copy(zz).wait_send()
+
+        @pl.when(zz != z)
+        def _():
+            up_copy(zz).wait_send()
+
+        for xx in range(2):
+            to_partner(zz, xx).wait_send()
+            answer_copy(zz, xx).wait_send()
+        return carry
+
+    lax.fori_loop(0, length, drain, 0)
+
+
+def gathered_plan(tokens, expert_ids, combine, gate_proj, up_proj, down_proj, capacity):
+    members = lax.axis_size("ep")
+    here, features = tokens.shape
+    ff = gate_proj.shape[1]
+    length = members // 4
+    experts = jnp.arange(members, dtype=jnp.int32)[:, None, None]
+    ids, shares = expert_ids.T[None], combine.T[None]
+    mix = jnp.sum(jnp.where(ids == experts, shares, 0.0), axis=1, keepdims=True)
+    block = (here, features)
+    dma = pltpu.SemaphoreType.DMA
+    vmem = lambda *shape: pltpu.VMEM(shape, jnp.bfloat16)
+    anywhere = pl.BlockSpec(memory_space=pl.ANY)
+    inside = pl.BlockSpec(memory_space=pltpu.VMEM)
+    return pl.pallas_call(
+        functools.partial(line_kernel, members=members, capacity=capacity),
+        out_shape=jax.ShapeDtypeStruct(block, jnp.bfloat16),
+        in_specs=[anywhere, inside, anywhere, anywhere, anywhere],
+        out_specs=inside,
+        scratch_shapes=[
+            vmem(length, 2, 2, *block),
+            pltpu.VMEM((members, 1, here), jnp.float32),
+            vmem(features, ff), vmem(features, ff), vmem(ff, features),
+            vmem(2 * capacity, features),
+            vmem(length, 2, *block), vmem(length, 2, *block), vmem(length, 2, *block),
+            vmem(length, *block), vmem(length, *block), vmem(length, *block),
+            dma((4,)), dma((length, 2)), dma((length,)), dma((length, 2)), dma((members,)),
+            dma((length, 2)), dma((length,)), dma((length,)),
+            dma((length, 2, 2)), dma((members,)), dma((length, 2)),
+            dma((length,)), dma((length,)), dma((length,)),
+        ],
+        compiler_params=pltpu.CompilerParams(
+            collective_id=0, has_side_effects=True, vmem_limit_bytes=60 * 1024 * 1024
+        ),
+    )(tokens, mix, gate_proj, up_proj, down_proj)
 
 
 def on_device(tokens, expert_ids, combine, gate_weight, up_weight, down_weight):
@@ -21,6 +322,10 @@
     features = tokens.shape[1]
     capacity = 2 * tokens_here * fanout // members
     received_rows = members * capacity
+    if members % 4 == 0 and 2 * capacity >= tokens_here:
+        return gathered_plan(
+            tokens, expert_ids, combine, gate_weight[0], up_weight[0], down_weight[0], capacity
+        )
     flat_ids = expert_ids.reshape(-1)
     onehot = (flat_ids[:, None] == jnp.arange(members, dtype=jnp.int32)[None, :]).astype(jnp.int32)
     running = jnp.cumsum(onehot, axis=0) - onehot

time: 204 us -> 119 us (0.58)
  the two profiles are of different devices: /device:TPU:8 before, /device:TPU:0 now
where the time goes in v1:
time: 119 us
  Pallas kernels  114 us (96%)
  local copies, waits for them, and re-layouts  3.81 us (3%)
  other arithmetic  1.3 us (1%)
    pallas_call x1, Pallas kernels, gathered_plan(): pl.pallas_call(functools.partial(line_kernel, members=members, capacity=c...  114 us

profile of v1, /device:TPU:0, one launch (start us, length us, event | category | flops | bytes accessed | tf_op | source)
XLA Modules:
  0.0 118.6 jit_solution(7844871065994680991)
XLA Ops:
  0.0 1.3 %select_reduce_fusion = f32[16,128]{1,0:T(8,128)} fusion(f32[4,128]{1,0:T(4,128)} %bitcast.10, s32[4,128]{1,0:T(4,128)} %bitcast.11), kind=kLoop, calls=%fused_computation | loop fusion | flops 22528 | bytes 12288 | tf_op jit(solution)/shard_map/reduce_sum | solution.py:290
  1.3 1.9 %copy.9.tok_hbm = bf16[128,1440]{1,0:T(8,128)(2,1)} copy(bf16[128,1440]{0,1:T(8,128)(2,1)} %param.6) | data formatting | bytes 737280 | tf_op args[0]
  3.2 113.5 %shard_map.64 = bf16[128,1440]{1,0:T(8,128)(2,1)} custom-call(bf16[128,1440]{1,0:T(8,128)(2,1)} %copy.9.tok_hbm, f32[16,1,128]{2,1,0:T(1,128)} %bitcast.9, bf16[1440,1440]{1,0:T(8,128)(2,1)} %bitcast.6, bf16[1440,1440]{1,0:T(8,128)(2,1)} %bitcast.7, bf16[1440,1440]{1,0:T(8,128)(2,1)} %bitcast.8), custom_call_target="tpu_custom_call" | custom-call | tf_op jit(solution)/shard_map/pallas_call | solution.py:296
  116.7 1.9 %copy.10 = bf16[128,1440]{0,1:T(8,128)(2,1)} copy(bf16[128,1440]{1,0:T(8,128)(2,1)} %shard_map.64) | data formatting | bytes 737280 | tf_op jit(solution)/shard_map/pallas_call | solution.py:296

commit v2 on v1

--- a/solution.py
+++ b/solution.py
@@ -175,6 +175,61 @@
             part[zz, xx].astype(jnp.float32) + quad[zz, xx].astype(jnp.float32)
         ).astype(jnp.bfloat16)
 
+    def up_copy(zz, xx):
+        return send(part.at[zz, xx], ru.at[zz, xx], rsz_s.at[zz, xx], ru_r.at[zz, xx], above)
+
+    def down_copy(zz, xx):
+        return send(part.at[zz, xx], rd.at[zz, xx], rsz_s.at[zz, xx], rd_r.at[zz, xx], below)
+
+    def add_in(zz, xx, addend):
+        part[zz, xx] = (
+            part[zz, xx].astype(jnp.float32) + addend.astype(jnp.float32)
+        ).astype(jnp.bfloat16)
+
+    def take_across(zz):
+        across_copy(zz).wait_recv()
+        add_in(zz, x, rx[zz])
+
+    def column(j):
+        return jnp.where(c == 1, x, (x + 1 + j) % 2)
+
+    def chain(zz):
+        @pl.when(c == 1)
+        def _():
+            take_across(zz)
+
+        def one(j, carry):
+            xx = column(j)
+
+            @pl.when(jnp.logical_and(zz >= z, z > 0))
+            def _():
+                up_copy(zz, xx).wait_recv()
+                add_in(zz, xx, ru[zz, xx])
+
+            @pl.when(jnp.logical_and(zz <= z, z < length - 1))
+            def _():
+                down_copy(zz, xx).wait_recv()
+                add_in(zz, xx, rd[zz, xx])
+
+            @pl.when(zz > z)
+            def _():
+                up_copy(zz, xx).start()
+
+            @pl.when(zz < z)
+            def _():
+                down_copy(zz, xx).start()
+
+            @pl.when(jnp.logical_and(zz == z, xx != x))
+            def _():
+                across_copy(zz).start()
+
+            return carry
+
+        lax.fori_loop(0, 2 - c, one, 0)
+
+    def starts(k):
+        return jnp.logical_and(near == 0, k >= 1)
+
     for load in loads[1:]:
         load.wait()
 
@@ -205,52 +260,43 @@
 
             @pl.when(o == 0)
             def _():
-                across_copy(last).start()
+                @pl.when(c == 1)
+                def _():
+                    across_copy(last).start()
+
+                @pl.when(jnp.logical_and(c == 0, starts(k - 1)))
+                def _():
+                    chain(last)
+
+        @pl.when(jnp.logical_and(jnp.logical_and(o == 1, c == 1), starts(k - 1)))
+        def _():
+            chain(nearest(k - 1))
 
         return carry
 
     lax.fori_loop(0, 2 * length, step_of, 0)
     final = nearest(length - 1)
     join_partner(final, 1 - x)
-    across_copy(final).start()
-
-    def up_copy(zz):
-        return send(part.at[zz, x], ru.at[zz], rsz_s.at[zz], ru_r.at[zz], above)
-
-    def down_copy(zz):
-        return send(part.at[zz, x], rd.at[zz], rsz_s.at[zz], rd_r.at[zz], below)
-
-    def chain(i, carry):
-        zz = nearest(length - 1 - i)
-        across_copy(zz).wait_recv()
-        total = part[zz, x].astype(jnp.float32) + rx[zz].astype(jnp.float32)
-        part[zz, x] = total.astype(jnp.bfloat16)
-
-        @pl.when(jnp.logical_and(zz >= z, z > 0))
-        def _():
-            up_copy(zz).wait_recv()
-            part[zz, x] = (
-                part[zz, x].astype(jnp.float32) + ru[zz].astype(jnp.float32)
-            ).astype(jnp.bfloat16)
-
-        @pl.when(jnp.logical_and(zz <= z, z < length - 1))
-        def _():
-            down_copy(zz).wait_recv()
-            part[zz, x] = (
-                part[zz, x].astype(jnp.float32) + rd[zz].astype(jnp.float32)
-            ).astype(jnp.bfloat16)
-
-        @pl.when(zz > z)
-        def _():
-            up_copy(zz).start()
-
-        @pl.when(zz < z)
-        def _():
-            down_copy(zz).start()
+
+    @pl.when(c == 1)
+    def _():
+        across_copy(final).start()
+
+    def rest(i, carry):
+        k = length - 1 - i
+
+        @pl.when(jnp.logical_not(starts(k)) | (k == length - 1))
+        def _():
+            chain(nearest(k))
 
         return carry
 
-    lax.fori_loop(0, length, chain, 0)
+    lax.fori_loop(0, length, rest, 0)
+
+    @pl.when(c == 0)
+    def _():
+        take_across(z)
+
     out_ref[...] = part[z, x]
 
     for step in range(1, members):
@@ -266,11 +312,18 @@
             to_below(zz).wait_send()
 
         to_across(zz).wait_send()
-        across_copy(zz).wait_send()
+
+        @pl.when(jnp.logical_or(c == 1, zz == z))
+        def _():
+            across_copy(zz).wait_send()
 
         @pl.when(zz != z)
         def _():
-            up_copy(zz).wait_send()
+            def one(j, inner):
+                up_copy(zz, column(j)).wait_send()
+                return inner
+
+            lax.fori_loop(0, 2 - c, one, 0)
 
         for xx in range(2):
             to_partner(zz, xx).wait_send()
@@ -304,11 +357,11 @@
             vmem(features, ff), vmem(features, ff), vmem(ff, features),
             vmem(2 * capacity, features),
             vmem(length, 2, *block), vmem(length, 2, *block), vmem(length, 2, *block),
-            vmem(length, *block), vmem(length, *block), vmem(length, *block),
+            vmem(length, *block), vmem(length, 2, *block), vmem(length, 2, *block),
             dma((4,)), dma((length, 2)), dma((length,)), dma((length, 2)), dma((members,)),
-            dma((length, 2)), dma((length,)), dma((length,)),
+            dma((length, 2)), dma((length,)), dma((length, 2)),
             dma((length, 2, 2)), dma((members,)), dma((length, 2)),
-            dma((length,)), dma((length,)), dma((length,)),
+            dma((length,)), dma((length, 2)), dma((length, 2)),
         ],
         compiler_params=pltpu.CompilerParams(
             collective_id=0, has_side_effects=True, vmem_limit_bytes=60 * 1024 * 1024

time: 119 us -> 120 us (level)
  the two profiles are of different devices: /device:TPU:0 before, /device:TPU:8 now
where the time goes in v2:
time: 120 us
  Pallas kernels  115 us (96%)
  local copies, waits for them, and re-layouts  3.81 us (3%)
  other arithmetic  1.3 us (1%)
    pallas_call x1, Pallas kernels, gathered_plan(): pl.pallas_call(functools.partial(line_kernel, members=members, capacity=c...  115 us

profile of v2, /device:TPU:8, one launch (start us, length us, event | category | flops | bytes accessed | tf_op | source)
XLA Modules:
  0.0 119.7 jit_solution(4570935521559762739)
XLA Ops:
  0.0 1.3 %select_reduce_fusion = f32[16,128]{1,0:T(8,128)} fusion(f32[4,128]{1,0:T(4,128)} %bitcast.10, s32[4,128]{1,0:T(4,128)} %bitcast.11), kind=kLoop, calls=%fused_computation | loop fusion | flops 22528 | bytes 12288 | tf_op jit(solution)/shard_map/reduce_sum | solution.py:343
  1.3 1.9 %copy.9.tok_hbm = bf16[128,1440]{1,0:T(8,128)(2,1)} copy(bf16[128,1440]{0,1:T(8,128)(2,1)} %param.6) | data formatting | bytes 737280 | tf_op args[0]
  3.2 114.6 %shard_map.64 = bf16[128,1440]{1,0:T(8,128)(2,1)} custom-call(bf16[128,1440]{1,0:T(8,128)(2,1)} %copy.9.tok_hbm, f32[16,1,128]{2,1,0:T(1,128)} %bitcast.9, bf16[1440,1440]{1,0:T(8,128)(2,1)} %bitcast.6, bf16[1440,1440]{1,0:T(8,128)(2,1)} %bitcast.7, bf16[1440,1440]{1,0:T(8,128)(2,1)} %bitcast.8), custom_call_target="tpu_custom_call" | custom-call | tf_op jit(solution)/shard_map/pallas_call | solution.py:349
  117.8 1.9 %copy.10 = bf16[128,1440]{0,1:T(8,128)(2,1)} copy(bf16[128,1440]{1,0:T(8,128)(2,1)} %shard_map.64) | data formatting | bytes 737280 | tf_op jit(solution)/shard_map/pallas_call | solution.py:349

commit v3 on v2

--- a/solution.py
+++ b/solution.py
@@ -25,8 +25,8 @@
     tok_hbm, mix_ref, gate_hbm, up_hbm, down_hbm, out_ref,
     x_buf, w_in, gate_w, up_w, down_w, rows, part, other, quad, rx, ru, rd,
     load_sem, agz_s, agx_s, agp_s, w_s, pc_s, rsx_s, rsz_s,
-    x_r, w_r, q_r, rx_r, ru_r, rd_r,
-    *, members, capacity,
+    x_r, xp_r, w_r, q_r, rx_r, ru_r, rd_r,
+    *, members, capacity, pieces,
 ):
     length = members // 4
     here = tok_hbm.shape[0]
@@ -71,21 +71,27 @@
         origin = lax.rem(me + step, members)
         return send(mix_ref.at[origin], w_in.at[origin], w_s.at[step], w_r.at[origin], origin)
 
-    def ag(zz, xx, ssem, to):
+    size = here // pieces
+
+    def cut(piece):
+        return pl.ds(pl.multiple_of(piece * size, size), size)
+
+    def ag(zz, piece, ssem, to):
+        slot = x_buf.at[zz, x, c, cut(piece)]
+        return send(slot, slot, ssem, x_r.at[zz, x, piece], to)
+
+    def to_above(zz, piece):
+        return ag(zz, piece, agz_s.at[zz, 0, piece], above)
+
+    def to_below(zz, piece):
+        return ag(zz, piece, agz_s.at[zz, 1, piece], below)
+
+    def to_across(zz, piece):
+        return ag(zz, piece, agx_s.at[zz, piece], across)
+
+    def to_partner(zz, xx):
         slot = x_buf.at[zz, xx, c]
-        return send(slot, slot, ssem, x_r.at[zz, xx, c], to)
-
-    def to_above(zz):
-        return ag(zz, x, agz_s.at[zz, 0], above)
-
-    def to_below(zz):
-        return ag(zz, x, agz_s.at[zz, 1], below)
-
-    def to_across(zz):
-        return ag(zz, x, agx_s.at[zz], across)
-
-    def to_partner(zz, xx):
-        return ag(zz, xx, agp_s.at[zz, xx], partner)
+        return send(slot, slot, agp_s.at[zz, xx], xp_r.at[zz, xx], partner)
 
     def goes_up(zz):
         return jnp.logical_and(zz <= z, z < length - 1)
@@ -93,21 +99,38 @@
     def goes_down(zz):
         return jnp.logical_and(zz >= z, z > 0)
 
-    def forward(zz):
-        @pl.when(goes_up(zz))
-        def _():
-            to_above(zz).start()
-
-        @pl.when(goes_down(zz))
-        def _():
-            to_below(zz).start()
-
-        to_across(zz).start()
+    def each_piece(act):
+        def one(piece, carry):
+            act(piece)
+            return carry
+
+        lax.fori_loop(0, pieces, one, 0)
+
+    def forward(zz, arriving):
+        def one(piece):
+            if arriving:
+                arrival(zz, x, piece)
+
+            @pl.when(goes_up(zz))
+            def _():
+                to_above(zz, piece).start()
+
+            @pl.when(goes_down(zz))
+            def _():
+                to_below(zz, piece).start()
+
+            to_across(zz, piece).start()
+
+        each_piece(one)
         to_partner(zz, x).start()
 
-    def arrival(zz, xx, cc):
-        slot = x_buf.at[zz, xx, cc]
-        send(slot, slot, agx_s.at[zz], x_r.at[zz, xx, cc], partner).wait_recv()
+    def arrival(zz, xx, piece):
+        slot = x_buf.at[zz, xx, c, cut(piece)]
+        send(slot, slot, agx_s.at[zz, piece], x_r.at[zz, xx, piece], partner).wait_recv()
+
+    def partner_arrival(zz, xx):
+        slot = x_buf.at[zz, xx, pc]
+        send(slot, slot, agp_s.at[zz, xx], xp_r.at[zz, xx], partner).wait_recv()
 
     near = jnp.minimum(z, length - 1 - z)
 
@@ -117,7 +140,7 @@
         return jnp.where(z == near, low, length - 1 - low)
 
     loads[0].wait()
-    forward(z)
+    forward(z, False)
     for step in range(1, members):
         weights_copy(step).start()
     w_in[me] = mix_ref[me]
@@ -166,8 +189,14 @@
     def answer_copy(zz, xx):
         return send(other.at[zz, xx], quad.at[zz, xx], pc_s.at[zz, xx], q_r.at[zz, xx], partner)
 
-    def across_copy(zz):
-        return send(part.at[zz, 1 - x], rx.at[zz], rsx_s.at[zz], rx_r.at[zz], across)
+    def across_copy(zz, piece):
+        return send(
+            part.at[zz, 1 - x, cut(piece)], rx.at[zz, cut(piece)],
+            rsx_s.at[zz, piece], rx_r.at[zz, piece], across,
+        )
+
+    def all_across(zz):
+        each_piece(lambda piece: across_copy(zz, piece).start())
 
     def join_partner(zz, xx):
         answer_copy(zz, xx).wait_recv()
@@ -175,57 +204,63 @@
             part[zz, xx].astype(jnp.float32) + quad[zz, xx].astype(jnp.float32)
         ).astype(jnp.bfloat16)
 
-    def up_copy(zz, xx):
-        return send(part.at[zz, xx], ru.at[zz, xx], rsz_s.at[zz, xx], ru_r.at[zz, xx], above)
-
-    def down_copy(zz, xx):
-        return send(part.at[zz, xx], rd.at[zz, xx], rsz_s.at[zz, xx], rd_r.at[zz, xx], below)
-
-    def add_in(zz, xx, addend):
-        part[zz, xx] = (
-            part[zz, xx].astype(jnp.float32) + addend.astype(jnp.float32)
+    def up_copy(zz, xx, piece):
+        return send(
+            part.at[zz, xx, cut(piece)], ru.at[zz, xx, cut(piece)],
+            rsz_s.at[zz, xx, piece], ru_r.at[zz, xx, piece], above,
+        )
+
+    def down_copy(zz, xx, piece):
+        return send(
+            part.at[zz, xx, cut(piece)], rd.at[zz, xx, cut(piece)],
+            rsz_s.at[zz, xx, piece], rd_r.at[zz, xx, piece], below,
+        )
+
+    def add_in(zz, xx, piece, addend):
+        part[zz, xx, cut(piece)] = (
+            part[zz, xx, cut(piece)].astype(jnp.float32) + addend.astype(jnp.float32)
         ).astype(jnp.bfloat16)
 
-    def take_across(zz):
-        across_copy(zz).wait_recv()
-        add_in(zz, x, rx[zz])
+    def take_across(zz, piece):
+        across_copy(zz, piece).wait_recv()
+        add_in(zz, x, piece, rx[zz, cut(piece)])
 
     def column(j):
         return jnp.where(c == 1, x, (x + 1 + j) % 2)
 
     def chain(zz):
-        @pl.when(c == 1)
-        def _():
-            take_across(zz)
-
-        def one(j, carry):
-            xx = column(j)
+        def one(step, carry):
+            xx, piece = column(step // pieces), step % pieces
+
+            @pl.when(c == 1)
+            def _():
+                take_across(zz, piece)
 
             @pl.when(jnp.logical_and(zz >= z, z > 0))
             def _():
-                up_copy(zz, xx).wait_recv()
-                add_in(zz, xx, ru[zz, xx])
+                up_copy(zz, xx, piece).wait_recv()
+                add_in(zz, xx, piece, ru[zz, xx, cut(piece)])
 
             @pl.when(jnp.logical_and(zz <= z, z < length - 1))
             def _():
-                down_copy(zz, xx).wait_recv()
-                add_in(zz, xx, rd[zz, xx])
+                down_copy(zz, xx, piece).wait_recv()
+                add_in(zz, xx, piece, rd[zz, xx, cut(piece)])
 
             @pl.when(zz > z)
             def _():
-                up_copy(zz, xx).start()
+                up_copy(zz, xx, piece).start()
 
             @pl.when(zz < z)
             def _():
-                down_copy(zz, xx).start()
+                down_copy(zz, xx, piece).start()
 
             @pl.when(jnp.logical_and(zz == z, xx != x))
             def _():
-                across_copy(zz).start()
+                across_copy(zz, piece).start()
 
             return carry
 
-        lax.fori_loop(0, 2 - c, one, 0)
+        lax.fori_loop(0, (2 - c) * pieces, one, 0)
 
     def starts(k):
         return jnp.logical_and(near == 0, k >= 1)
@@ -242,13 +277,12 @@
             @pl.when(k + 1 < length)
             def _():
                 following = nearest(k + 1)
-                arrival(following, x, c)
-                forward(following)
-
-            arrival(zz, 1 - x, c)
+                forward(following, True)
+
+            each_piece(lambda piece: arrival(zz, 1 - x, piece))
             to_partner(zz, 1 - x).start()
 
-        arrival(zz, xx, pc)
+        partner_arrival(zz, xx)
         compute(zz, xx)
         answer_copy(zz, xx).start()
 
@@ -262,7 +296,7 @@
             def _():
                 @pl.when(c == 1)
                 def _():
-                    across_copy(last).start()
+                    all_across(last)
 
                 @pl.when(jnp.logical_and(c == 0, starts(k - 1)))
                 def _():
@@ -272,6 +306,10 @@
         def _():
             chain(nearest(k - 1))
 
+        @pl.when(jnp.logical_and(near == 1, i == 2 * length - 1))
+        def _():
+            chain(nearest(1))
+
         return carry
 
     lax.fori_loop(0, 2 * length, step_of, 0)
@@ -280,12 +318,16 @@
 
     @pl.when(c == 1)
     def _():
-        across_copy(final).start()
+        all_across(final)
 
     def rest(i, carry):
         k = length - 1 - i
 
-        @pl.when(jnp.logical_not(starts(k)) | (k == length - 1))
+        early = jnp.logical_or(
+            jnp.logical_and(starts(k), k < length - 1), jnp.logical_and(near == 1, k == 1)
+        )
+
+        @pl.when(jnp.logical_not(early))
         def _():
             chain(nearest(k))
 
@@ -295,7 +337,7 @@
 
     @pl.when(c == 0)
     def _():
-        take_across(z)
+        each_piece(lambda piece: take_across(z, piece))
 
     out_ref[...] = part[z, x]
 
@@ -303,28 +345,30 @@
         weights_copy(step).wait_send()
 
     def drain(zz, carry):
-        @pl.when(goes_up(zz))
-        def _():
-            to_above(zz).wait_send()
-
-        @pl.when(goes_down(zz))
-        def _():
-            to_below(zz).wait_send()
-
-        to_across(zz).wait_send()
-
-        @pl.when(jnp.logical_or(c == 1, zz == z))
-        def _():
-            across_copy(zz).wait_send()
-
-        @pl.when(zz != z)
-        def _():
-            def one(j, inner):
-                up_copy(zz, column(j)).wait_send()
-                return inner
-
-            lax.fori_loop(0, 2 - c, one, 0)
-
+        def one(piece):
+            @pl.when(goes_up(zz))
+            def _():
+                to_above(zz, piece).wait_send()
+
+            @pl.when(goes_down(zz))
+            def _():
+                to_below(zz, piece).wait_send()
+
+            to_across(zz, piece).wait_send()
+
+            @pl.when(jnp.logical_or(c == 1, zz == z))
+            def _():
+                across_copy(zz, piece).wait_send()
+
+            @pl.when(zz != z)
+            def _():
+                up_copy(zz, x, piece).wait_send()
+
+            @pl.when(jnp.logical_and(zz != z, c == 0))
+            def _():
+                up_copy(zz, 1 - x, piece).wait_send()
+
+        each_piece(one)
         for xx in range(2):
             to_partner(zz, xx).wait_send()
             answer_copy(zz, xx).wait_send()
@@ -338,6 +382,7 @@
     here, features = tokens.shape
     ff = gate_proj.shape[1]
     length = members // 4
+    pieces = 4 if here % 64 == 0 else 1
     experts = jnp.arange(members, dtype=jnp.int32)[:, None, None]
     ids, shares = expert_ids.T[None], combine.T[None]
     mix = jnp.sum(jnp.where(ids == experts, shares, 0.0), axis=1, keepdims=True)
@@ -347,7 +392,7 @@
     anywhere = pl.BlockSpec(memory_space=pl.ANY)
     inside = pl.BlockSpec(memory_space=pltpu.VMEM)
     return pl.pallas_call(
-        functools.partial(line_kernel, members=members, capacity=capacity),
+        functools.partial(line_kernel, members=members, capacity=capacity, pieces=pieces),
         out_shape=jax.ShapeDtypeStruct(block, jnp.bfloat16),
         in_specs=[anywhere, inside, anywhere, anywhere, anywhere],
         out_specs=inside,
@@ -358,10 +403,11 @@
             vmem(2 * capacity, features),
             vmem(length, 2, *block), vmem(length, 2, *block), vmem(length, 2, *block),
             vmem(length, *block), vmem(length, 2, *block), vmem(length, 2, *block),
-            dma((4,)), dma((length, 2)), dma((length,)), dma((length, 2)), dma((members,)),
-            dma((length, 2)), dma((length,)), dma((length, 2)),
-            dma((length, 2, 2)), dma((members,)), dma((length, 2)),
-            dma((length,)), dma((length, 2)), dma((length, 2)),
+            dma((4,)), dma((length, 2, pieces)), dma((length, pieces)), dma((length, 2)),
+            dma((members,)),
+            dma((length, 2)), dma((length, pieces)), dma((length, 2, pieces)),
+            dma((length, 2, pieces)), dma((length, 2)), dma((members,)), dma((length, 2)),
+            dma((length, pieces)), dma((length, 2, pieces)), dma((length, 2, pieces)),
         ],
         compiler_params=pltpu.CompilerParams(
             collective_id=0, has_side_effects=True, vmem_limit_bytes=60 * 1024 * 1024

time: 120 us -> 105 us (0.88); the launches traced: 120 us -> 103 us
  Pallas kernels: 115 us -> 98.2 us
    pallas_call x1, Pallas kernels: 115 us -> 98.2 us  [gathered_plan(): pl.pallas_call(functools.partial(line_kernel, members=members, capacity=c...]
where the time goes in v3:
time: 105 us; the launch traced here: 103 us
  Pallas kernels  98.2 us (94%)
  local copies, waits for them, and re-layouts  3.81 us (4%)
  other arithmetic  1.3 us (1%)
    pallas_call x1, Pallas kernels, gathered_plan(): pl.pallas_call(functools.partial(line_kernel, members=members, capacity=c...  98.2 us

profile of v3, /device:TPU:8, one launch (start us, length us, event | category | flops | bytes accessed | tf_op | source)
XLA Modules:
  0.0 103.3 jit_solution(16899333361671157024)
XLA Ops:
  0.0 1.3 %select_reduce_fusion = f32[16,128]{1,0:T(8,128)} fusion(f32[4,128]{1,0:T(4,128)} %bitcast.10, s32[4,128]{1,0:T(4,128)} %bitcast.11), kind=kLoop, calls=%fused_computation | loop fusion | flops 22528 | bytes 12288 | tf_op jit(solution)/shard_map/reduce_sum | solution.py:388
  1.3 1.9 %copy.9.tok_hbm = bf16[128,1440]{1,0:T(8,128)(2,1)} copy(bf16[128,1440]{0,1:T(8,128)(2,1)} %param.6) | data formatting | bytes 737280 | tf_op args[0]
  3.2 98.2 %shard_map.64 = bf16[128,1440]{1,0:T(8,128)(2,1)} custom-call(bf16[128,1440]{1,0:T(8,128)(2,1)} %copy.9.tok_hbm, f32[16,1,128]{2,1,0:T(1,128)} %bitcast.9, bf16[1440,1440]{1,0:T(8,128)(2,1)} %bitcast.6, bf16[1440,1440]{1,0:T(8,128)(2,1)} %bitcast.7, bf16[1440,1440]{1,0:T(8,128)(2,1)} %bitcast.8), custom_call_target="tpu_custom_call" | custom-call | tf_op jit(solution)/shard_map/pallas_call | solution.py:394
  101.4 1.9 %copy.10 = bf16[128,1440]{0,1:T(8,128)(2,1)} copy(bf16[128,1440]{1,0:T(8,128)(2,1)} %shard_map.64) | data formatting | bytes 737280 | tf_op jit(solution)/shard_map/pallas_call | solution.py:394
